TPU v7x, 256 devices: a 8x8x2 block of a 8x8x16 slice. The times are simulated.
256 devices in a mesh: grp: 2 (over z), pool: 128 (over y, x, core).
Axes of the slice: x: 8, y: 8, z: 2, core: 2. Of those that a mesh axis runs over, the one named last changes fastest.
The devices are a block of a 8x8x16 slice.
Arguments:
- query: bfloat16 [256, 4096], P(('grp', 'pool')), parts along dimension 0, may hold values from -6 to 6
- kv_pool: bfloat16 [16384, 2, 16, 512], P(('grp', 'pool')), parts along dimension 0, may hold values from -6 to 6
- holder_table: int32 [256, 128], P(('grp', 'pool')), parts along dimension 0, may hold values from 0 to 127, as said below
- slot_table: int32 [256, 128], P(('grp', 'pool')), parts along dimension 0, may hold values from 0 to 63
- lengths: int32 [256], P(('grp', 'pool')), parts along dimension 0, may hold values from 96 to 128, as said below
- out_weight: bfloat16 [4096, 8192], P('pool'), may hold values from -5 to 5
Outputs:
- mixed: bfloat16 [256, 8192], P(('grp', 'pool')), parts along dimension 0
There are 2 independent parts, one for each index of `grp`. A program takes and returns all parts, laid end to end along the dimension named above; an argument that names none is the same for every part. Nothing has to cross between parts.
Inputs may be any that keep to these rules, and one draw needn't show every extreme that they name: `holder_table`: entry [r, j] is the index along pool of the device holding block j of request r. Of one request's 128 blocks at most 2 have the same holder, and some holder has exactly 2 of the request's first 96 blocks. Request r's live blocks are 0 to lengths[r] - 1; some request has 128.
All inputs are finite; a program needn't handle non-finite values.
Results may differ from a plain program's by a relative error of at most 0.0053.
Values may be sent and summed in bfloat16 or wider, within the bound.
No kernel may reach another device: no remote copies, remote signals or barrier semaphores. Data moves between devices by JAX's collectives and lax.ppermute only.
A program may use at most 64 MiB of HBM per device.

v0:
```python
import math
import jax
import jax.numpy as jnp
from jax import lax
from jax.sharding import Mesh
from jax.sharding import PartitionSpec as P

H = 32
KVH = 4
HD = 128
POOL = ("pool_0", "pool_1", "pool_2")
GRP_POOL = ("grp", "pool_0", "pool_1", "pool_2")
lowest = -1e30


def side_by_side(arrays, axis, dim, along):
    columns = [a.reshape(*a.shape[:along], -1) for a in arrays]
    both = jnp.concatenate(columns, axis=along)
    out, at, outs = (lax.all_gather(both, axis, axis=dim, tiled=True), 0, [])
    for a, column in zip(arrays, columns):
        piece = out[..., at : at + column.shape[along]]
        outs.append(piece.reshape(*piece.shape[:along], *a.shape[along:]))
        at += column.shape[along]
    return tuple(outs)


def side_by_side_2(arrays, axis, split_dim, concat_dim, along):
    widths = [a.shape[along] for a in arrays]
    both = jnp.concatenate(arrays, axis=along)
    out = lax.all_to_all(both, axis, split_axis=split_dim, concat_axis=concat_dim, tiled=True)
    return tuple(jnp.split(out, [sum(widths[:k]) for k in range(1, len(widths))], axis=along))


def laid_out(pieces, dim):
    lengths = list(pieces.shape[1:])
    lengths[dim] *= pieces.shape[0]
    return jnp.moveaxis(pieces, 0, dim).reshape(lengths)


def gather_in_order(x, axes, order):
    pieces = x[None]
    for k in order:
        pieces = lax.all_gather(pieces, axes[k], axis=0, tiled=True)
    block = [lax.axis_size(axes[k]) for k in reversed(order)]
    pieces = pieces.reshape(*block, *x.shape)
    turned = sorted(range(len(order)), key=lambda place: order[len(order) - 1 - place])
    return pieces.transpose(*turned, *range(len(order), pieces.ndim)).reshape(-1, *x.shape)


def gathered_by_axis(x, axes, order, dim):
    return laid_out(gather_in_order(x, axes, order), dim)


def block_partials(query_heads, kv_blocks):
    head_dim = query_heads.shape[-1]
    kv_heads = query_heads.shape[1]
    block_len = kv_blocks.shape[3]
    block_shape = kv_blocks.shape[:2] + (block_len, kv_heads, head_dim)
    key_part = kv_blocks[:, :, 0].reshape(block_shape)
    value_part = kv_blocks[:, :, 1].reshape(block_shape)
    scores = jnp.einsum(
        "agqd,acbgd->acgqb", query_heads, key_part, preferred_element_type=jnp.float32
    )
    scores = scores * (1.0 / math.sqrt(head_dim))
    maxima = jnp.max(scores, axis=-1)
    shifted = jnp.exp(scores - maxima[..., None])
    totals = jnp.sum(shifted, axis=-1)
    outputs = jnp.einsum(
        "acgqb,acbgd->acgqd",
        shifted.astype(jnp.bfloat16),
        value_part,
        preferred_element_type=jnp.float32,
    )
    return (maxima, outputs, totals)


def merge_blocks(maxima, outputs, totals, live_mask, axis_pos):
    peak_score = jnp.max(jnp.where(live_mask, maxima, lowest), axis=axis_pos, keepdims=True)
    factor = jnp.exp(jnp.where(live_mask, maxima - peak_score, lowest))
    numerator = jnp.sum(factor[..., None] * outputs, axis=axis_pos)
    denominator = jnp.sum(factor * totals, axis=axis_pos)
    return (jnp.squeeze(peak_score, axis_pos), numerator, denominator)


def per_device(query, kv_pool, holder_table, slot_table, lengths, out_weight):
    pool_size = lax.axis_size(POOL)
    my_index = lax.axis_index(POOL)
    max_blocks = holder_table.shape[1]
    capacity = 2 * max_blocks // pool_size
    groups = H // KVH
    all_holders, all_slots, all_lengths = side_by_side(
        (holder_table, slot_table, lengths), POOL, 0, 1
    )
    cap_iota = jnp.arange(capacity, dtype=jnp.int32)
    block_iota = jnp.arange(max_blocks, dtype=jnp.int32)
    held_here = all_holders == my_index
    rank_here = jnp.cumsum(held_here.astype(jnp.int32), axis=1) - 1
    pick_hot = held_here[:, None, :] & (rank_here[:, None, :] == cap_iota[None, :, None])
    pick_slot = jnp.sum(jnp.where(pick_hot, all_slots[:, None, :], 0), axis=-1)
    pick_block = jnp.sum(jnp.where(pick_hot, block_iota[None, None, :], 0), axis=-1)
    send_live = jnp.any(pick_hot, axis=-1) & (pick_block < all_lengths[:, None])
    send_blocks = kv_pool[pick_slot]
    all_queries = lax.all_gather(query, POOL, axis=0, tiled=True)
    maxima, outputs, totals = block_partials(
        all_queries.reshape(pool_size, KVH, groups, HD), send_blocks
    )
    part_peak, part_numer, part_denom = merge_blocks(
        maxima, outputs, totals, send_live[:, :, None, None], 1
    )
    got_peak, got_numer, got_denom = side_by_side_2(
        (
            part_peak.reshape(pool_size, H),
            part_numer.reshape(pool_size, H * HD),
            part_denom.reshape(pool_size, H),
        ),
        POOL,
        0,
        0,
        1,
    )
    peak_score, numerator, denominator = merge_blocks(
        got_peak.reshape(pool_size, KVH, groups),
        got_numer.reshape(pool_size, KVH, groups, HD),
        got_denom.reshape(pool_size, KVH, groups),
        True,
        0,
    )
    attention = (numerator / denominator[..., None]).reshape(1, H * HD).astype(jnp.bfloat16)
    weight_block = lax.all_to_all(out_weight, POOL, split_axis=1, concat_axis=0, tiled=True)
    every_request = gathered_by_axis(attention, POOL, (0, 1, 2), 0)
    column_part = jnp.dot(every_request, weight_block, preferred_element_type=jnp.float32).astype(
        jnp.bfloat16
    )
    mixed = lax.all_to_all(column_part, POOL, split_axis=0, concat_axis=1, tiled=True)
    return mixed


def solution(mesh):
    torus = Mesh(
        mesh.devices.reshape(mesh.shape["grp"], 8, 8, 2), ("grp", "pool_0", "pool_1", "pool_2")
    )
    return jax.shard_map(
        per_device,
        mesh=torus,
        in_specs=(
            P(GRP_POOL, None),
            P(GRP_POOL, None, None, None),
            P(GRP_POOL, None),
            P(GRP_POOL, None),
            P(GRP_POOL),
            P(POOL, None),
        ),
        out_specs=P(GRP_POOL, None),
        check_vma=False,
    )
```

profile of v0, /device:TPU:513, one launch (start us, length us, event | category | flops | bytes accessed | tf_op | source)
XLA Modules:
  0.0 358.0 jit_solution(3321120689761888645)
XLA Ops:
  6.6 0.7 all-gather.7.cloned.1.call-update
  8.7 67.2 %all-gather = s32[128,1,257]{2,1,0:T(1,128)S(1)} all-gather(s32[1,1,257]{2,1,0:T(1,128)S(1)} %add_bitcast_fusion), channel_id=1, replica_groups=mesh['grp'=2,'pool_0'=8,'pool_1'=8,'pool_2'=2] {'pool_0','pool_1','pool_2'}, dimensions={0}, use_global_device_ids=true | all-gather | bytes 132612 | tf_op jit(solution)/shard_map/all_gather | solution.py:19
  77.0 8.8 %gather_fusion = bf16[256,2,16,512]{3,2,1,0:T(8,128)(2,1)} fusion(bf16[64,2,16,512]{3,2,1,0:T(8,128)(2,1)S(1)} %copy-done, s32[1024]{0:T(1024)S(1)} %pad_clamp_fusion), kind=kCustom, calls=%fused_computation | custom fusion | bytes 16778240 | tf_op jit(solution)/shard_map/gather | solution.py:102
  85.8 6.4 %fusion.10 = (bf16[128,2,1,16,512]{4,3,2,1,0:T(8,128)(2,1)}, bf16[128,2,1,16,512]{4,3,2,1,0:T(8,128)(2,1)}) fusion(bf16[128,2,2,16,512]{4,3,2,1,0:T(8,128)(2,1)} %bitcast.61), kind=kLoop, calls=%fused_computation.34 | loop fusion | bytes 16777216 | tf_op jit(solution)/shard_map/slice | solution.py:60
  92.3 7.9 %copy.129 = bf16[128,2,1,16,512]{0,4,3,1,2:T(8,128)(2,1)} copy(bf16[128,2,1,16,512]{4,3,2,1,0:T(8,128)(2,1)} %get-tuple-element.12) | data formatting | bytes 8388608 | tf_op jit(solution)/shard_map/slice | solution.py:59
  100.2 8.0 %copy.131 = bf16[128,2,16,4,128]{4,2,1,3,0:T(8,128)(2,1)} copy(bf16[128,2,16,4,128]{0,4,3,2,1:T(8,128)(2,1)} %bitcast.62) | data formatting | bytes 8388608 | tf_op jit(solution)/shard_map/reshape;squeeze | solution.py:59
  108.2 7.9 %copy.138 = bf16[128,2,1,16,512]{0,4,3,1,2:T(8,128)(2,1)} copy(bf16[128,2,1,16,512]{4,3,2,1,0:T(8,128)(2,1)} %get-tuple-element.11) | data formatting | bytes 8388608 | tf_op jit(solution)/shard_map/slice | solution.py:60
  116.0 7.9 %copy.140 = bf16[128,2,16,4,128]{4,2,3,1,0:T(8,128)(2,1)} copy(bf16[128,2,16,4,128]{0,4,3,2,1:T(8,128)(2,1)} %bitcast.63) | data formatting | bytes 8388608 | tf_op jit(solution)/shard_map/reshape;squeeze | solution.py:60
  124.1 5.0 %copy.130 = bf16[128,1,4096]{0,2,1:T(8,128)(2,1)S(1)} copy(bf16[128,1,4096]{2,1,0:T(2,128)(2,1)} %all-gather.7.cloned.1.call-done) | data formatting | bytes 2097152 | tf_op jit(solution)/shard_map/all_gather | solution.py:103
  129.2 1.0 copy.150
  130.2 14.0 %fusion.11 = f32[128,4,2,16,8]{3,4,2,1,0:T(8,128)} fusion(bf16[128,2,16,4,128]{4,2,1,3,0:T(8,128)(2,1)} %copy.131, bf16[128,4,8,128,1]{3,2,4,1,0:T(8,128)(2,1)S(1)} %copy.150), kind=kOutput, calls=%fused_computation.36 | convolution fusion | flops 33554432 | bytes 5767168 | tf_op jit(solution)/shard_map/agqd,acbgd->acgqb/dot_general | solution.py:61
  144.2 3.7 %copy.133 = f32[128,4,2,16,8]{0,3,4,1,2:T(8,128)S(1)} copy(f32[128,4,2,16,8]{3,4,2,1,0:T(8,128)} %fusion.11) | data formatting | bytes 1048576 | tf_op jit(solution)/shard_map/agqd,acbgd->acgqb/dot_general | solution.py:61
  148.5 3.0 copy.139
  151.4 4.9 %multiply_reduce_fusion = f32[128,4,8,128]{3,2,1,0:T(8,128)} fusion(bf16[128,2,4,8,16]{4,3,2,1,0:T(8,128)(2,1)S(1)} %copy.139, bf16[128,2,16,4,128]{4,2,3,1,0:T(8,128)(2,1)} %copy.140, f32[128,2,4,8]{3,2,1,0:T(4,128)S(1)} %copy.137), kind=kOutput, calls=%fused_computation.1 | convolution fusion | flops 35127296 | bytes 6586368 | tf_op jit(solution)/shard_map/acgqb,acbgd->acgqd/dot_general | solution.py:68
  156.4 2.0 copy.153
  158.4 1.4 maximum_bitcast_fusion
  159.8 5.7 %copy.144 = f32[128,1,4160]{2,1,0:T(1,128)} copy(f32[128,1,4160]{0,2,1:T(8,128)} %maximum_bitcast_fusion) | data formatting | bytes 4259840 | tf_op jit(solution)/shard_map/all_to_all | solution.py:30
  165.5 60.6 %all_to_all.47 = f32[128,1,4160]{2,1,0:T(1,128)} all-to-all(f32[128,1,4160]{2,1,0:T(1,128)} %copy.144), channel_id=1, replica_groups=mesh['grp'=2,'pool_0'=8,'pool_1'=8,'pool_2'=2] {'pool_0','pool_1','pool_2'}, dimensions={0} | all-to-all | bytes 4259840 | tf_op jit(solution)/shard_map/all_to_all | solution.py:30
  226.1 5.7 %copy.145 = f32[128,1,4160]{0,2,1:T(8,128)} copy(f32[128,1,4160]{2,1,0:T(1,128)} %all_to_all.47) | data formatting | bytes 4259840 | tf_op jit(solution)/shard_map/all_to_all | solution.py:30
  231.8 0.9 slice_reduce_fusion
  232.6 0.9 fusion.7
  233.7 0.8 fusion.8
  234.5 2.2 fusion
  236.9 18.6 %all_gather.17 = bf16[8,1,4096]{2,1,0:T(2,128)(2,1)S(1)} all-gather(bf16[1,1,4096]{2,1,0:T(2,128)(2,1)S(1)} %divide_convert_fusion), channel_id=1, replica_groups=mesh['grp'=2,'pool_0'=8,'pool_1'=8,'pool_2'=2] {'pool_0'}, dimensions={0}, use_global_device_ids=true | all-gather | bytes 73728 | tf_op jit(solution)/shard_map/all_gather | solution.py:43
  255.6 21.6 %all_gather.18 = bf16[64,1,4096]{2,0,1:T(8,128)(2,1)} all-gather(bf16[8,1,4096]{2,0,1:T(8,128)(2,1)S(1)} %copy.146), channel_id=1, replica_groups=mesh['grp'=2,'pool_0'=8,'pool_1'=8,'pool_2'=2] {'pool_1'}, dimensions={0}, use_global_device_ids=true | all-gather | bytes 589824 | tf_op jit(solution)/shard_map/all_gather | solution.py:43
  277.2 1.1 all_to_all.37
  279.6 42.9 %all_to_all.48 = bf16[128,2,1024]{2,1,0:T(2,128)(2,1)S(1)} all-to-all(bf16[128,2,1024]{2,1,0:T(2,128)(2,1)S(1)} %reshape.145), channel_id=1, replica_groups=mesh['grp'=2,'pool_0'=8,'pool_1'=8,'pool_2'=2] {'pool_0','pool_1','pool_2'}, dimensions={0} | all-to-all | bytes 1048576 | tf_op jit(solution)/shard_map/all_to_all | solution.py:129
  323.2 3.5 copy.147
  326.7 2.3 reshape_reshape.3
  328.9 1.8 fusion.1
  330.8 19.4 %all_to_all.49 = bf16[128,1,64]{2,1,0:T(2,128)(2,1)S(1)} all-to-all(bf16[128,1,64]{2,1,0:T(2,128)(2,1)S(1)} %copy.149), channel_id=1, replica_groups=mesh['grp'=2,'pool_0'=8,'pool_1'=8,'pool_2'=2] {'pool_0','pool_1','pool_2'}, dimensions={0} | all-to-all | bytes 32768 | tf_op jit(solution)/shard_map/all_to_all | solution.py:134
  350.4 0.7 all_to_all.43
  (43 shorter events, 5.1 us)
Async XLA Ops:
  6.5 70.5 %copy-start = (bf16[64,2,16,512]{3,2,1,0:T(8,128)(2,1)S(1)}, bf16[64,2,16,512]{3,2,1,0:T(8,128)(2,1)}, u32[]{:S(2)}) copy-start(bf16[64,2,16,512]{3,2,1,0:T(8,128)(2,1)} %param.7) | copy-start | bytes 6291460
  6.6 117.6 %all-gather.7.cloned.1.call-start = ((), (), s32[]{:S(2)}) async-start(), calls=%async_computation.4 | async-start | bytes 2113536 | tf_op jit(solution)/shard_map/all_gather | solution.py:103
  7.3 315.9 %all-gather.5.cloned.1.call-start = ((), (), s32[]{:S(2)}) async-start(), calls=%async_computation.3 | async-start | bytes 1572864 | tf_op jit(solution)/shard_map/all_gather | solution.py:43
  231.8 45.5 %copy-start.2 = (bf16[32,8192]{1,0:T(8,128)(2,1)S(1)}, bf16[32,8192]{1,0:T(8,128)(2,1)}, u32[]{:S(2)}) copy-start(bf16[32,8192]{1,0:T(8,128)(2,1)} %param.11) | copy-start | bytes 1572868
  323.2 27.9 %copy-start.1 = (bf16[64,2,16,512]{3,2,1,0:T(8,128)(2,1)S(1)}, bf16[64,2,16,512]{3,2,1,0:T(8,128)(2,1)}, u32[]{:S(2)}) copy-start(bf16[64,2,16,512]{3,2,1,0:T(8,128)(2,1)} %param.7) | copy-start | bytes 6291460
Sparse Core Ops, SparseCore 0:
  9.9 98.6 all-gather.6
  277.3 31.8 all-gather.4
where the time goes:
time: 360 us; the launch traced here: 358 us
  blocking collectives  230 us (64%)
  local copies, waits for them, and re-layouts  83.9 us (23%)
  matrix products  20.7 us (6%)
  between operations  14.3 us (4%)
  other arithmetic  7.94 us (2%)
    all_gather x1, blocking collectives, side_by_side(): out, at, outs = (lax.all_gather(both, axis, axis=dim, tiled=True), 0, [])  67.2 us
    all_to_all x1, blocking collectives, side_by_side_2(): lax.all_to_all(both, axis, split_axis=split_dim, concat_axis=concat_dim,...  60.6 us
    all_to_all x1, blocking collectives, per_device(): lax.all_to_all(out_weight, POOL, split_axis=1, concat_axis=0, tiled=True)  42.9 us
    all_gather x2, blocking collectives, gather_in_order(): pieces = lax.all_gather(pieces, axes[k], axis=0, tiled=True)  40.2 us
    all_to_all x1, blocking collectives, per_device(): lax.all_to_all(column_part, POOL, split_axis=0, concat_axis=1, tiled=True)  19.4 us
    slice x2, local copies, waits for them, and re-layouts, block_partials(): value_part = kv_blocks[:, :, 1].reshape(block_shape)  14.3 us
    dot_general x1, matrix products, block_partials(): jnp.einsum('agqd,acbgd->acgqb', query_heads, key_part, preferred_element_...  14 us
    all_to_all x2, local copies, waits for them, and re-layouts, side_by_side_2(): lax.all_to_all(both, axis, split_axis=split_dim, concat_axis=concat_dim,...  11.4 us
  transfers between devices with their start and end apart: 2, of which 0 were waited for; matrix products, arithmetic and copies ran while one was open for 14% of the time, Pallas kernels for 0%

commit v1 on v0

--- a/solution.py
+++ b/solution.py
@@ -40,7 +40,13 @@
 def gather_in_order(x, axes, order):
     pieces = x[None]
     for k in order:
-        pieces = lax.all_gather(pieces, axes[k], axis=0, tiled=True)
+        take_the_chunk = lambda w_in, mesh_name: jnp.concatenate(
+            jax.lax.all_to_all(
+                jnp.stack([w_in for _ in range(jax.lax.axis_size(mesh_name))], 0), mesh_name, 0, 0
+            ),
+            axis=0,
+        )
+        pieces = take_the_chunk(pieces, axes[k])
     block = [lax.axis_size(axes[k]) for k in reversed(order)]
     pieces = pieces.reshape(*block, *x.shape)
     turned = sorted(range(len(order)), key=lambda place: order[len(order) - 1 - place])

time: 360 us -> 342 us (0.950)
  blocking collectives: 230 us -> 153 us
  waiting for transfers between devices: 0.84 us -> 40.1 us
  starting transfers between devices: 0.06 us -> 17.8 us
    all_gather x2 -> x0, blocking collectives: 40.2 us -> none  [gather_in_order(): pieces = lax.all_gather(pieces, axes[k], axis=0, tiled=True)]
    all_to_all x0 -> x3, waiting for transfers between devices: none -> 39.3 us  [the longest x2 19.9 us: gather_in_order(): jax.lax.all_to_all(jnp.stack([w_in for _ in range(jax.lax.axis_size(mesh_...]
    all_to_all x1, blocking collectives: 42.9 us -> 5.97 us  [gather_in_order(): jax.lax.all_to_all(jnp.stack([w_in for _ in range(jax.lax.axis_size(mesh_...]
    all_to_all x0 -> x3, starting transfers between devices: none -> 17.8 us  [the longest x1 9.82 us: per_device(): lax.all_to_all(out_weight, POOL, split_axis=1, concat_axis=0, tiled=True)]
  transfers between devices with their start and end apart: 2 -> 4, of which waited for: 0 -> 3; matrix products, arithmetic and copies ran while one was open for 14% -> 15% of each run, Pallas kernels for 0% -> 0%
where the time goes in v1:
time: 342 us; the launch traced here: 340 us
  blocking collectives  153 us (45%)
  local copies, waits for them, and re-layouts  85.5 us (25%)
  waiting for transfers between devices  40.1 us (12%)
  matrix products  20.7 us (6%)
  starting transfers between devices  17.8 us (5%)
  between operations  14.3 us (4%)
  other arithmetic  9.09 us (3%)
    all_gather x1, blocking collectives, side_by_side(): out, at, outs = (lax.all_gather(both, axis, axis=dim, tiled=True), 0, [])  67.2 us
    all_to_all x1, blocking collectives, side_by_side_2(): lax.all_to_all(both, axis, split_axis=split_dim, concat_axis=concat_dim,...  60.6 us
    all_to_all x2, waiting for transfers between devices, gather_in_order(): jax.lax.all_to_all(jnp.stack([w_in for _ in range(jax.lax.axis_size(mesh_...  19.9 us
    all_to_all x1, waiting for transfers between devices, per_device(): lax.all_to_all(out_weight, POOL, split_axis=1, concat_axis=0, tiled=True)  19.4 us
    all_to_all x1, blocking collectives, per_device(): lax.all_to_all(column_part, POOL, split_axis=0, concat_axis=1, tiled=True)  19.1 us
    slice x2, local copies, waits for them, and re-layouts, block_partials(): value_part = kv_blocks[:, :, 1].reshape(block_shape)  14.3 us
    dot_general x1, matrix products, block_partials(): jnp.einsum('agqd,acbgd->acgqb', query_heads, key_part, preferred_element_...  14 us
    all_to_all x2, local copies, waits for them, and re-layouts, side_by_side_2(): lax.all_to_all(both, axis, split_axis=split_dim, concat_axis=concat_dim,...  11.4 us
  transfers between devices with their start and end apart: 4, of which 3 were waited for; matrix products, arithmetic and copies ran while one was open for 15% of the time, Pallas kernels for 0%

profile of v1, /device:TPU:513, one launch (start us, length us, event | category | flops | bytes accessed | tf_op | source)
XLA Modules:
  0.0 340.4 jit_solution(5574051132559374880)
XLA Ops:
  8.6 67.2 %all-gather = s32[128,1,257]{2,1,0:T(1,128)S(1)} all-gather(s32[1,1,257]{2,1,0:T(1,128)S(1)} %add_bitcast_fusion), channel_id=1, replica_groups=mesh['grp'=2,'pool_0'=8,'pool_1'=8,'pool_2'=2] {'pool_0','pool_1','pool_2'}, dimensions={0}, use_global_device_ids=true | all-gather | bytes 132612 | tf_op jit(solution)/shard_map/all_gather | solution.py:19
  77.0 8.8 %gather_fusion = bf16[256,2,16,512]{3,2,1,0:T(8,128)(2,1)} fusion(bf16[64,2,16,512]{3,2,1,0:T(8,128)(2,1)S(1)} %copy-done, s32[1024]{0:T(1024)S(1)} %pad_clamp_fusion), kind=kCustom, calls=%fused_computation | custom fusion | bytes 16778240 | tf_op jit(solution)/shard_map/gather | solution.py:108
  85.7 6.4 %fusion.11 = (bf16[128,2,1,16,512]{4,3,2,1,0:T(8,128)(2,1)}, bf16[128,2,1,16,512]{4,3,2,1,0:T(8,128)(2,1)}) fusion(bf16[128,2,2,16,512]{4,3,2,1,0:T(8,128)(2,1)} %bitcast.68), kind=kLoop, calls=%fused_computation.38 | loop fusion | bytes 16777216 | tf_op jit(solution)/shard_map/slice | solution.py:66
  92.2 7.9 %copy.125 = bf16[128,2,1,16,512]{0,4,3,1,2:T(8,128)(2,1)} copy(bf16[128,2,1,16,512]{4,3,2,1,0:T(8,128)(2,1)} %get-tuple-element.12) | data formatting | bytes 8388608 | tf_op jit(solution)/shard_map/slice | solution.py:65
  100.1 8.0 %copy.127 = bf16[128,2,16,4,128]{4,2,1,3,0:T(8,128)(2,1)} copy(bf16[128,2,16,4,128]{0,4,3,2,1:T(8,128)(2,1)} %bitcast.69) | data formatting | bytes 8388608 | tf_op jit(solution)/shard_map/reshape;squeeze | solution.py:65
  108.1 7.9 %copy.134 = bf16[128,2,1,16,512]{0,4,3,1,2:T(8,128)(2,1)} copy(bf16[128,2,1,16,512]{4,3,2,1,0:T(8,128)(2,1)} %get-tuple-element.11) | data formatting | bytes 8388608 | tf_op jit(solution)/shard_map/slice | solution.py:66
  116.0 7.9 %copy.136 = bf16[128,2,16,4,128]{4,2,3,1,0:T(8,128)(2,1)} copy(bf16[128,2,16,4,128]{0,4,3,2,1:T(8,128)(2,1)} %bitcast.70) | data formatting | bytes 8388608 | tf_op jit(solution)/shard_map/reshape;squeeze | solution.py:66
  124.1 5.0 %copy.126 = bf16[128,1,4096]{0,2,1:T(8,128)(2,1)S(1)} copy(bf16[128,1,4096]{2,1,0:T(2,128)(2,1)} %all-gather.4.cloned.1.call-done) | data formatting | bytes 2097152 | tf_op jit(solution)/shard_map/all_gather | solution.py:109
  130.1 14.0 %fusion.12 = f32[128,4,2,16,8]{3,4,2,1,0:T(8,128)} fusion(bf16[128,2,16,4,128]{4,2,1,3,0:T(8,128)(2,1)} %copy.127, bf16[128,4,8,128,1]{3,2,4,1,0:T(8,128)(2,1)S(1)} %copy.145), kind=kOutput, calls=%fused_computation.40 | convolution fusion | flops 33554432 | bytes 5767168 | tf_op jit(solution)/shard_map/agqd,acbgd->acgqb/dot_general | solution.py:67
  144.1 3.7 %copy.129 = f32[128,4,2,16,8]{0,3,4,1,2:T(8,128)S(1)} copy(f32[128,4,2,16,8]{3,4,2,1,0:T(8,128)} %fusion.12) | data formatting | bytes 1048576 | tf_op jit(solution)/shard_map/agqd,acbgd->acgqb/dot_general | solution.py:67
  148.4 3.0 copy.135
  151.4 4.9 %multiply_reduce_fusion = f32[128,4,8,128]{3,2,1,0:T(8,128)} fusion(bf16[128,2,4,8,16]{4,3,2,1,0:T(8,128)(2,1)S(1)} %copy.135, bf16[128,2,16,4,128]{4,2,3,1,0:T(8,128)(2,1)} %copy.136, f32[128,2,4,8]{3,2,1,0:T(4,128)S(1)} %copy.133), kind=kOutput, calls=%fused_computation.1 | convolution fusion | flops 35127296 | bytes 6586368 | tf_op jit(solution)/shard_map/acgqb,acbgd->acgqd/dot_general | solution.py:74
  156.3 2.0 copy.148
  158.3 1.4 maximum_bitcast_fusion
  159.8 5.7 %copy.140 = f32[128,1,4160]{2,1,0:T(1,128)} copy(f32[128,1,4160]{0,2,1:T(8,128)} %maximum_bitcast_fusion) | data formatting | bytes 4259840 | tf_op jit(solution)/shard_map/all_to_all | solution.py:30
  165.5 60.6 %all_to_all.62 = f32[128,1,4160]{2,1,0:T(1,128)} all-to-all(f32[128,1,4160]{2,1,0:T(1,128)} %copy.140), channel_id=1, replica_groups=mesh['grp'=2,'pool_0'=8,'pool_1'=8,'pool_2'=2] {'pool_0','pool_1','pool_2'}, dimensions={0} | all-to-all | bytes 4259840 | tf_op jit(solution)/shard_map/all_to_all | solution.py:30
  226.1 5.7 %copy.141 = f32[128,1,4160]{0,2,1:T(8,128)} copy(f32[128,1,4160]{2,1,0:T(1,128)} %all_to_all.62) | data formatting | bytes 4259840 | tf_op jit(solution)/shard_map/all_to_all | solution.py:30
  234.5 2.2 fusion
  237.4 1.0 reduce.4
  239.1 4.3 %all-to-all-start.1 = ((bf16[8,2,2048]{2,1,0:T(2,128)(2,1)}), bf16[8,2,2048]{2,1,0:T(2,128)(2,1)S(1)}, u32[]{:S(2)}, u32[]{:S(2)}) async-start(bf16[8,2,2048]{2,1,0:T(2,128)(2,1)} %reshape.140), calls=%async_computation.1 | async-start | bytes 131072 | tf_op jit(solution)/shard_map/all_to_all | solution.py:44
  243.4 1.1 all_to_all.49
  245.2 1.4 reshape.142
  246.6 4.0 %all-to-all-done.1 = bf16[8,2,2048]{2,1,0:T(2,128)(2,1)S(1)} async-done(((bf16[8,2,2048]{2,1,0:T(2,128)(2,1)}), bf16[8,2,2048]{2,1,0:T(2,128)(2,1)S(1)}, u32[]{:S(2)}, u32[]{:S(2)}) %all-to-all-start.1) | async-done | bytes 65568 | tf_op jit(solution)/shard_map/all_to_all | solution.py:44
  250.6 9.8 %all-to-all-start.4 = ((bf16[128,2,1024]{2,1,0:T(2,128)(2,1)}), bf16[128,2,1024]{2,1,0:T(2,128)(2,1)S(1)}, u32[]{:S(2)}, u32[]{:S(2)}) async-start(bf16[128,2,1024]{2,1,0:T(2,128)(2,1)} %reshape.142), calls=%async_computation.4 | async-start | bytes 1048576 | tf_op jit(solution)/shard_map/all_to_all | solution.py:135
  260.6 19.4 %all-to-all-done.4 = bf16[128,2,1024]{2,1,0:T(2,128)(2,1)S(1)} async-done(((bf16[128,2,1024]{2,1,0:T(2,128)(2,1)}), bf16[128,2,1024]{2,1,0:T(2,128)(2,1)S(1)}, u32[]{:S(2)}, u32[]{:S(2)}) %all-to-all-start.4) | async-done | bytes 524320 | tf_op jit(solution)/shard_map/all_to_all | solution.py:135
  280.8 3.7 %all-to-all-start.2 = ((bf16[8,8,1,4096]{3,1,2,0:T(8,128)(2,1)}), bf16[8,8,1,4096]{3,1,2,0:T(8,128)(2,1)S(1)}, u32[]{:S(2)}, u32[]{:S(2)}) async-start(bf16[8,8,1,4096]{3,1,2,0:T(8,128)(2,1)} %stack.10), calls=%async_computation.2 | async-start | bytes 1048576 | tf_op jit(solution)/shard_map/all_to_all | solution.py:44
  285.1 15.9 %all-to-all-done.2 = bf16[8,8,1,4096]{3,1,2,0:T(8,128)(2,1)S(1)} async-done(((bf16[8,8,1,4096]{3,1,2,0:T(8,128)(2,1)}), bf16[8,8,1,4096]{3,1,2,0:T(8,128)(2,1)S(1)}, u32[]{:S(2)}, u32[]{:S(2)}) %all-to-all-start.2) | async-done | bytes 524320 | tf_op jit(solution)/shard_map/all_to_all | solution.py:44
  301.1 6.0 %all_to_all.63 = bf16[2,64,1,4096]{3,1,2,0:T(8,128)(2,1)S(1)} all-to-all(bf16[2,64,1,4096]{3,1,2,0:T(8,128)(2,1)S(1)} %pad_maximum_fusion), channel_id=1, replica_groups=mesh['grp'=2,'pool_0'=8,'pool_1'=8,'pool_2'=2] {'pool_2'}, dimensions={0} | all-to-all | bytes 2097152 | tf_op jit(solution)/shard_map/all_to_all | solution.py:44
  307.1 2.1 copy.155
  309.2 2.4 reshape_reshape.7
  311.6 1.8 fusion.1
  313.5 19.1 %all_to_all.64 = bf16[128,1,64]{2,1,0:T(2,128)(2,1)S(1)} all-to-all(bf16[128,1,64]{2,1,0:T(2,128)(2,1)S(1)} %copy.144), channel_id=1, replica_groups=mesh['grp'=2,'pool_0'=8,'pool_1'=8,'pool_2'=2] {'pool_0','pool_1','pool_2'}, dimensions={0} | all-to-all | bytes 32768 | tf_op jit(solution)/shard_map/all_to_all | solution.py:140
  (50 shorter events, 11.6 us)
Async XLA Ops:
  6.5 70.4 %copy-start = (bf16[64,2,16,512]{3,2,1,0:T(8,128)(2,1)S(1)}, bf16[64,2,16,512]{3,2,1,0:T(8,128)(2,1)}, u32[]{:S(2)}) copy-start(bf16[64,2,16,512]{3,2,1,0:T(8,128)(2,1)} %param.7) | copy-start | bytes 6291460
  6.6 117.5 %all-gather.4.cloned.1.call-start = ((), (), s32[]{:S(2)}) async-start(), calls=%async_computation.6 | async-start | bytes 2113536 | tf_op jit(solution)/shard_map/all_gather | solution.py:109
  231.7 11.6 %copy-start.2 = (bf16[32,8192]{1,0:T(8,128)(2,1)S(1)}, bf16[32,8192]{1,0:T(8,128)(2,1)}, u32[]{:S(2)}) copy-start(bf16[32,8192]{1,0:T(8,128)(2,1)} %param.11) | copy-start | bytes 1572868
  239.1 11.5 %all-to-all-start.1 = ((bf16[8,2,2048]{2,1,0:T(2,128)(2,1)}), bf16[8,2,2048]{2,1,0:T(2,128)(2,1)S(1)}, u32[]{:S(2)}, u32[]{:S(2)}) async-start(bf16[8,2,2048]{2,1,0:T(2,128)(2,1)} %reshape.140), calls=%async_computation.1 | async-start | bytes 131072 | tf_op jit(solution)/shard_map/all_to_all | solution.py:44
  250.6 29.4 %all-to-all-start.4 = ((bf16[128,2,1024]{2,1,0:T(2,128)(2,1)}), bf16[128,2,1024]{2,1,0:T(2,128)(2,1)S(1)}, u32[]{:S(2)}, u32[]{:S(2)}) async-start(bf16[128,2,1024]{2,1,0:T(2,128)(2,1)} %reshape.142), calls=%async_computation.4 | async-start | bytes 1048576 | tf_op jit(solution)/shard_map/all_to_all | solution.py:135
  280.8 20.2 %all-to-all-start.2 = ((bf16[8,8,1,4096]{3,1,2,0:T(8,128)(2,1)}), bf16[8,8,1,4096]{3,1,2,0:T(8,128)(2,1)S(1)}, u32[]{:S(2)}, u32[]{:S(2)}) async-start(bf16[8,8,1,4096]{3,1,2,0:T(8,128)(2,1)} %stack.10), calls=%async_computation.2 | async-start | bytes 1048576 | tf_op jit(solution)/shard_map/all_to_all | solution.py:44
  309.2 24.3 %copy-start.1 = (bf16[64,2,16,512]{3,2,1,0:T(8,128)(2,1)S(1)}, bf16[64,2,16,512]{3,2,1,0:T(8,128)(2,1)}, u32[]{:S(2)}) copy-start(bf16[64,2,16,512]{3,2,1,0:T(8,128)(2,1)} %param.7) | copy-start | bytes 6291460
Sparse Core Ops, SparseCore 0:
  9.9 98.6 all-gather.3
